TPU v7x, 256 devices: a whole 4x4x8 slice. The times are simulated.
256 devices in a mesh: node: 16 (over z, core), group: 16 (over x, y).
Axes of the slice: x: 4, y: 4, z: 8, core: 2. Of those that a mesh axis runs over, the one named last changes fastest.
Arguments:
- gradient: bfloat16 [16, 16, 1024, 1024], P('node', 'group'), may hold values from -60 to 60
- momentum: float32 [1024, 1024], replicated, may hold values from -6 to 6
- variance: float32 [1024, 1024], replicated, may hold values from 0.004 to 0.4
- params: float32 [1024, 1024], replicated, may hold values from -6 to 6
- worker_error: float32 [16, 16, 1024, 1024], P('node', 'group'), may hold values from -18 to 18, as said below
- server_error: float32 [16, 1024, 1024], P('group', 'node'), may hold values from -12 to 12, as said below
- group_worker_error: float32 [16, 1024, 1024], P('group', 'node'), may hold values from -12 to 12, as said below
- group_server_error: float32 [1024, 1024], P(('node', 'group')), may hold values from -12 to 12, as said below
Outputs:
- new_params: float32 [1024, 1024], replicated
- new_momentum: float32 [1024, 1024], replicated
- new_worker_error: float32 [16, 16, 1024, 1024], P('node', 'group')
- new_server_error: float32 [16, 1024, 1024], P('group', 'node')
- new_group_worker_error: float32 [16, 1024, 1024], P('group', 'node')
- new_group_server_error: float32 [1024, 1024], P(('node', 'group'))
Inputs may be any that keep to these rules, and one draw needn't show every extreme that they name: `worker_error`: no entry of local has magnitude under 0.005. No entry of group_mean + server_error has magnitude under 0.005. No entry of group_q + group_worker_error has magnitude under 0.005. No entry of total_mean + group_server_error has magnitude under 0.005.
All inputs are finite; a program needn't handle non-finite values.
Results may differ from a plain program's by a relative error of at most 0.0003.
Values sent between devices are 32-bit elements; how exact they have to be, the bound alone decides.
A program may use at most 128 MiB of HBM per device.

v0:
```python
import jax
import jax.numpy as jnp
from jax import lax
from jax.sharding import PartitionSpec as P


def joined_along(pieces, dim):
    shape = list(pieces.shape[1:])
    shape[dim] *= pieces.shape[0]
    return jnp.moveaxis(pieces, 0, dim).reshape(shape)


def from_everyone(x, axis):
    devices = lax.axis_size(axis)
    return lax.all_to_all(jnp.broadcast_to(x[None], (devices, *x.shape)), axis, 0, 0, tiled=True)


def gather_directly(x, axis, dim):
    return joined_along(from_everyone(x, axis), dim)


def compress(values):
    scale = jnp.mean(jnp.abs(values), axis=-1, keepdims=True)
    packed = scale * jnp.sign(values)
    return (packed, values - packed)


def body(
    gradient,
    momentum,
    variance,
    params,
    worker_error,
    server_error,
    group_worker_error,
    group_server_error,
):
    nodes = lax.axis_size("node")
    groups = lax.axis_size("group")
    rows = momentum.shape[0]
    width = momentum.shape[1]
    shard_rows = rows // nodes
    local = 0.9 * momentum + 0.1 * gradient[0, 0].astype(jnp.float32) + worker_error[0, 0]
    first, new_worker_error = compress(local)
    arrived = lax.all_to_all(
        first.reshape(nodes, shard_rows, width), "node", split_axis=0, concat_axis=0, tiled=True
    )
    group_mean = jnp.sum(arrived, axis=0) / nodes
    group_q, new_server_error = compress(group_mean + server_error[0])
    second, new_group_worker_error = compress(group_q + group_worker_error[0])
    received = lax.all_to_all(
        second.reshape(groups, shard_rows // groups, width),
        "group",
        split_axis=0,
        concat_axis=0,
        tiled=True,
    )
    total_mean = jnp.sum(received, axis=0) / groups
    piece_momentum, new_group_server_error = compress(total_mean + group_server_error)
    shard_momentum = gather_directly(piece_momentum, "group", 0)
    new_momentum = lax.all_gather(shard_momentum, "node", axis=0, tiled=True)
    new_params = params - 0.05 * new_momentum / (jnp.sqrt(variance) + 1e-08)
    return (
        new_params,
        new_momentum,
        new_worker_error[None, None],
        new_server_error[None],
        new_group_worker_error[None],
        new_group_server_error,
    )


def solution(mesh):
    in_specs = (
        P("node", "group", None, None),
        P(),
        P(),
        P(),
        P("node", "group", None, None),
        P("group", "node", None),
        P("group", "node", None),
        P(("node", "group"), None),
    )
    out_specs = (
        P(),
        P(),
        P("node", "group", None, None),
        P("group", "node", None),
        P("group", "node", None),
        P(("node", "group"), None),
    )
    return jax.shard_map(body, mesh=mesh, in_specs=in_specs, out_specs=out_specs, check_vma=False)
```

profile of v0, /device:TPU:1, one launch (start us, length us, event | category | flops | bytes accessed | tf_op | source)
XLA Modules:
  0.0 209.2 jit_solution(3343924632842586397)
XLA Ops:
  7.2 5.1 %abs_reduce_fusion = (f32[1024]{0:T(1024)S(1)}, f32[1024,1024]{1,0:T(8,128)S(1)}) fusion(f32[1,1,1024,1024]{3,2,1,0:T(8,128)} %param.12, bf16[1,1,1024,1024]{3,2,1,0:T(8,128)(2,1)} %param.8, f32[1024,1024]{1,0:T(8,128)} %param.9), kind=kLoop, calls=%fused_computation.5 | loop fusion | flops 7339008 | bytes 14684160 | tf_op jit(solution)/shard_map/reduce_sum | solution.py:23
  12.2 4.6 %subtract_bitcast_fusion = (f32[1,1,1024,1024]{3,2,1,0:T(8,128)}, f32[1024,1024]{1,0:T(8,128)}) fusion(f32[1024,1024]{1,0:T(8,128)S(1)} %get-tuple-element.7, f32[1024]{0:T(1024)S(1)} %broadcast_multiply_fusion.1), kind=kLoop, calls=%fused_computation.2 | loop fusion | flops 3145728 | bytes 12587008 | tf_op jit(solution)/shard_map/broadcast_in_dim | solution.py:66
  16.9 0.0 copy-start.1
  16.9 0.0 copy-start.2
  16.9 10.1 %all-to-all-start = ((f32[16,64,1024]{2,1,0:T(8,128)}), f32[16,64,1024]{2,1,0:T(8,128)}, u32[]{:S(2)}, u32[]{:S(2)}) async-start(f32[16,64,1024]{2,1,0:T(8,128)} %bitcast.29), calls=%async_computation | async-start | bytes 8388608 | tf_op jit(solution)/shard_map/all_to_all | solution.py:45
  27.0 0.0 all-gather.2.cloned.1.call-start
  27.0 0.0 copy-done.1
  27.0 0.1 squeeze.17
  27.1 0.0 copy-done.2
  27.1 0.1 squeeze.18
  27.2 0.0 copy-start.3
  27.2 93.3 %all-to-all-done = f32[16,64,1024]{2,1,0:T(8,128)} async-done(((f32[16,64,1024]{2,1,0:T(8,128)}), f32[16,64,1024]{2,1,0:T(8,128)}, u32[]{:S(2)}, u32[]{:S(2)}) %all-to-all-start) | async-done | bytes 4194336 | tf_op jit(solution)/shard_map/all_to_all | solution.py:45
  120.5 2.5 %reduce_sum.55 = f32[64,1024]{1,0:T(8,128)S(1)} reduce(f32[16,64,1024]{2,1,0:T(8,128)} %all-to-all-done, f32[]{:T(128)} %constant.9.clone.1), dimensions={0}, to_apply=%region_1.0 | reduce | flops 983040 | bytes 4456452 | tf_op jit(solution)/shard_map/reduce_sum | solution.py:48
  123.0 0.1 abs_reduce_fusion.1
  123.1 0.2 fusion.1
  123.3 0.1 div.45
  123.4 0.1 div.44
  123.5 0.1 div.46
  123.6 0.3 sign_multiply_fusion.2
  123.9 14.0 %all_to_all.15 = f32[16,4,1024]{2,1,0:T(4,128)S(1)} all-to-all(f32[16,4,1024]{2,1,0:T(4,128)S(1)} %sign_multiply_fusion.2), channel_id=1, replica_groups=mesh['node'=16,'group'=16] {'group'}, dimensions={0} | all-to-all | bytes 524288 | tf_op jit(solution)/shard_map/all_to_all | solution.py:51
  137.9 0.1 reduce_sum.58
  138.0 0.0 copy-done.3
  138.0 0.1 abs_reduce_fusion.2
  138.1 0.7 fusion.3
  138.9 10.8 %all_to_all.16 = f32[16,4,1024]{2,1,0:T(4,128)S(1)} all-to-all(f32[16,4,1024]{2,1,0:T(4,128)S(1)} %broadcast_in_dim.4), channel_id=1, replica_groups=mesh['node'=16,'group'=16] {'group'}, dimensions={0} | all-to-all | bytes 524288 | tf_op jit(solution)/shard_map/all_to_all | solution.py:15
  149.6 0.8 reshape.92
  150.4 0.0 all-gather.2.cloned.1.call-update
  150.4 0.9 multiply_subtract_fusion
  151.3 40.1 %all-gather.2.cloned.1.call-done = f32[1024,1024]{1,0:T(8,128)} async-done(((f32[64,1024]{1,0:T(8,128)}), f32[1024,1024]{1,0:T(8,128)}) %all-gather.2.cloned.1.call-update) | async-done | bytes 4194320 | tf_op jit(solution)/shard_map/all_gather | solution.py:61
  191.5 0.0 copy-start
  191.5 8.9 %divide_subtract_fusion = f32[1024,1024]{1,0:T(8,128)} fusion(f32[1024,1024]{1,0:T(8,128)} %param.11, f32[1024,1024]{1,0:T(8,128)} %param.10, f32[1024,1024]{1,0:T(8,128)} %all-gather.2.cloned.1.call-done), kind=kLoop, calls=%fused_computation.3 | loop fusion | flops 4194304 | bytes 16777216 | tf_op jit(solution)/shard_map/sub | solution.py:62
  200.4 0.0 copy-done
  200.4 2.0 copy.15
  (5 shorter events, 0.1 us)
Async XLA Ops:
  16.9 10.2 %copy-start.1 = (f32[1,64,1024]{2,1,0:T(8,128)S(1)}, f32[1,64,1024]{2,1,0:T(8,128)}, u32[]{:S(2)}) copy-start(f32[1,64,1024]{2,1,0:T(8,128)} %param.13) | copy-start | bytes 786436
  16.9 10.2 %copy-start.2 = (f32[1,64,1024]{2,1,0:T(8,128)S(1)}, f32[1,64,1024]{2,1,0:T(8,128)}, u32[]{:S(2)}) copy-start(f32[1,64,1024]{2,1,0:T(8,128)} %param.14) | copy-start | bytes 786436
  16.9 103.6 %all-to-all-start = ((f32[16,64,1024]{2,1,0:T(8,128)}), f32[16,64,1024]{2,1,0:T(8,128)}, u32[]{:S(2)}, u32[]{:S(2)}) async-start(f32[16,64,1024]{2,1,0:T(8,128)} %bitcast.29), calls=%async_computation | async-start | bytes 8388608 | tf_op jit(solution)/shard_map/all_to_all | solution.py:45
  27.0 164.5 %all-gather.2.cloned.1.call-start = ((), (), s32[]{:S(2)}) async-start(), calls=%async_computation.3 | async-start | bytes 4456448 | tf_op jit(solution)/shard_map/all_gather | solution.py:61
  27.2 110.8 %copy-start.3 = (f32[4,1024]{1,0:T(4,128)S(1)}, f32[4,1024]{1,0:T(4,128)}, u32[]{:S(2)}) copy-start(f32[4,1024]{1,0:T(4,128)} %param.15) | copy-start | bytes 49156
  191.5 8.9 %copy-start = (f32[1024,1024]{1,0:T(8,128)S(1)}, f32[1024,1024]{1,0:T(8,128)}, u32[]{:S(2)}) copy-start(f32[1024,1024]{1,0:T(8,128)} %all-gather.2.cloned.1.call-done) | copy-start | bytes 12582916
Sparse Core Ops, SparseCore 0:
  150.6 40.8 all-gather.1
where the time goes:
time: 210 us; the launch traced here: 209 us
  waiting for transfers between devices  133 us (63%)
  blocking collectives  24.8 us (12%)
  other arithmetic  23.5 us (11%)
  between operations  14.1 us (7%)
  starting transfers between devices  10.1 us (5%)
  local copies, waits for them, and re-layouts  3.26 us (2%)
    all_to_all x1, waiting for transfers between devices, body(): lax.all_to_all(first.reshape(nodes, shard_rows, width), 'node', split_axi...  93.3 us
    all_gather x1, waiting for transfers between devices, body(): new_momentum = lax.all_gather(shard_momentum, 'node', axis=0, tiled=True)  40.1 us
    all_to_all x1, blocking collectives, body(): lax.all_to_all(second.reshape(groups, shard_rows // groups, width), 'grou...  14 us
    all_to_all x1, blocking collectives, from_everyone(): lax.all_to_all(jnp.broadcast_to(x[None], (devices, *x.shape)), axis, 0, 0...  10.8 us
    all_to_all x1, starting transfers between devices, body(): lax.all_to_all(first.reshape(nodes, shard_rows, width), 'node', split_axi...  10.1 us
    sub x1, other arithmetic, body(): new_params = params - 0.05 * new_momentum / (jnp.sqrt(variance) + 1e-08)  8.89 us
    reduce_sum x4, other arithmetic, compress(): scale = jnp.mean(jnp.abs(values), axis=-1, keepdims=True)  5.53 us
    broadcast_in_dim x1, other arithmetic, body(): new_worker_error[None, None]  4.62 us
  transfers between devices with their start and end apart: 2, of which 2 were waited for; matrix products, arithmetic and copies ran while one was open for 1% of the time, Pallas kernels for 0%

commit v1 on v0

v1 whole, which is shorter than its diff:
```python
import functools

import jax
import jax.numpy as jnp
from jax import lax
from jax.experimental import pallas as pl
from jax.experimental.pallas import tpu as pltpu
from jax.sharding import PartitionSpec as P

MESH = pl.DeviceIdType.MESH
NZ, NX, NY = 8, 4, 4
SHARD = 64
HALF = 32
WIDTH = 1024
PIECE = (8, 512)
OFFSETS = (4, -3, 3, -2, 2, -1, 1, 0)
SLOT = {offset: i for i, offset in enumerate(OFFSETS)}
DOWN = ((4, 0), (-3, 1), (-3, 0), (-2, 1), (-2, 0), (-1, 1), (-1, 0))
UP = ((4, 1), (3, 0), (3, 1), (2, 0), (2, 1), (1, 0), (1, 1))
F32 = jnp.float32


def mod(i, n):
    return lax.rem(i + n, n)


def rows_of(start, size):
    return pl.ds(pl.multiple_of(start, size), size)


def compress(values):
    scale = jnp.sum(jnp.abs(values), axis=1, keepdims=True) * (1.0 / WIDTH)
    packed = jnp.where(values >= 0.0, scale, -scale)
    return packed, values - packed


def kernel(
    grad_hbm, mom_hbm, var_hbm, par_hbm, we_hbm, se_hbm, gwe_hbm, gse_hbm,
    new_p, new_m, new_we, new_se, new_gwe, new_gse,
    gbuf, mbuf, webuf, pbuf, vbuf, sebuf, gwebuf, gsebuf,
    own, psend, precv, rbuf, secp, recvg, mp,
    ld_sem, ld2_sem, ps_sem, pr_sem, rs_send, rs_recv, ge_send, ge_recv,
    z_send, z_recv, b_send, b_recv, a_send, a_recv, d_send, d_recv,
):
    n = lax.axis_index("node")
    g = lax.axis_index("group")
    z, c = lax.div(n, 2), lax.rem(n, 2)
    x, y = lax.div(g, NY), lax.rem(g, NY)
    partner = (2 * z + 1 - c, g)
    sent = []

    def zdev(offset):
        return (2 * mod(z + offset, NZ) + c, g)

    def gdev(dx, dy):
        return (n, mod(x + dx, NX) * NY + mod(y + dy, NY))

    def remote(src, dst, ssem, rsem, device):
        copy = pltpu.make_async_remote_copy(
            src_ref=src, dst_ref=dst, send_sem=ssem, recv_sem=rsem,
            device_id=device, device_id_type=MESH,
        )
        return copy

    def send(src, dst, ssem, rsem, device):
        copy = remote(src, dst, ssem, rsem, device)
        copy.start()
        sent.append(copy)

    def arrived(dst, rsem):
        remote(dst, dst, rsem, rsem, partner).wait_recv()

    barrier = pltpu.get_barrier_semaphore()
    friends = [partner]
    friends += [zdev(o) for o in range(1, NZ)]
    friends += [(n, lax.rem(g + o, NX * NY)) for o in range(1, NX * NY)]
    for device in friends:
        pl.semaphore_signal(barrier, inc=1, device_id=device, device_id_type=MESH)

    loads = {}
    for i, offset in enumerate(OFFSETS):
        rows = rows_of(mod(z + offset, NZ) * (2 * SHARD), 2 * SHARD)
        loads[i] = [
            pltpu.make_async_copy(src.at[rows, :], buf.at[i], ld_sem.at[i, k])
            for k, (src, buf) in enumerate(
                ((grad_hbm, gbuf), (mom_hbm, mbuf), (we_hbm, webuf))
            )
        ]
        for load in loads[i]:
            load.start()
    late = [
        pltpu.make_async_copy(src, buf, ld2_sem.at[k])
        for k, (src, buf) in enumerate(
            ((var_hbm, vbuf), (par_hbm, pbuf), (se_hbm, sebuf), (gwe_hbm, gwebuf), (gse_hbm, gsebuf))
        )
    ]
    for load in late:
        load.start()

    def local_part(i, part, dst):
        zb = mod(z + OFFSETS[i], NZ)

        def step(t, carry):
            r = part * SHARD + t * HALF
            at = rows_of(r, HALF)
            local = 0.9 * mbuf[i, at, :] + 0.1 * gbuf[i, at, :].astype(F32) + webuf[i, at, :]
            packed, error = compress(local)
            dst[i, rows_of(t * HALF, HALF), :] = packed
            new_we[rows_of(zb * (2 * SHARD) + r, HALF), :] = error
            return carry

        lax.fori_loop(0, SHARD // HALF, step, 0)

    def local_block(i, first=False):
        for load in loads[i]:
            load.wait()
        local_part(i, 1 - c, psend)
        if first:
            pl.semaphore_wait(barrier, len(friends))
        send(psend.at[i], precv.at[i], ps_sem.at[i], pr_sem.at[i], partner)
        local_part(i, c, own)

    def half_rows(half):
        return pl.ds(half * HALF, HALF)

    def rs_step(direction, s):
        offset, half = (DOWN, UP)[direction][s]
        i, at = SLOT[offset], half_rows(half)
        device = zdev(-1 if direction == 0 else 1)
        dst = rbuf.at[direction, s]
        if s < 2:
            own[i, at, :] = own[i, at, :] + precv[i, at, :]
            src = own.at[i, at, :]
        else:
            src = rbuf.at[direction, s - 2]
            arrived(src, rs_recv.at[direction, s - 2])
            rbuf[direction, s - 2] = rbuf[direction, s - 2] + (own[i, at, :] + precv[i, at, :])
        send(src, dst, rs_send.at[direction, s], rs_recv.at[direction, s], device)

    def partner_here(i):
        arrived(precv.at[i], pr_sem.at[i])

    local_block(0, first=True)
    partner_here(0)
    rs_step(0, 0)
    rs_step(1, 0)
    local_block(1)
    local_block(2)
    partner_here(1)
    rs_step(0, 1)
    partner_here(2)
    rs_step(1, 1)
    for i in range(3, 8):
        local_block(i)
    for load in late:
        load.wait()
    for i in range(3, 8):
        partner_here(i)

    def coefficients(first, count):
        def step(t, carry):
            at = rows_of(t * HALF, HALF)
            vbuf[at, :] = 0.05 / (jnp.sqrt(vbuf[at, :]) + 1e-8)
            return carry

        lax.fori_loop(first, first + count, step, 0)

    for s in range(2, 7):
        rs_step(0, s)
        rs_step(1, s)
        if s < 6:
            coefficients((s - 2) * 8, 8)

    low = lax.broadcasted_iota(jnp.int32, PIECE, 0) < 4
    last = SLOT[0]
    for half, (down_s, up_s) in ((0, (6, 5)), (1, (5, 6))):
        at = half_rows(half)
        arrived(rbuf.at[0, down_s], rs_recv.at[0, down_s])
        arrived(rbuf.at[1, up_s], rs_recv.at[1, up_s])
        total = own[last, at, :] + precv[last, at, :] + rbuf[0, down_s] + rbuf[1, up_s]
        group_q, error = compress(total * (1.0 / 16.0) + sebuf[at, :])
        new_se[at, :] = error
        second, error = compress(group_q + gwebuf[at, :])
        new_gwe[at, :] = error
        for t in range(HALF // 8):
            left, right = second[8 * t : 8 * t + 8, :512], second[8 * t : 8 * t + 8, 512:]
            k = half * 8 + 2 * t
            secp[k] = jnp.where(low, left, pltpu.roll(right, 4, 0))
            secp[k + 1] = jnp.where(low, pltpu.roll(left, 4, 0), right)

    for o in range(1, NX * NY):
        to = lax.rem(g + o, NX * NY)
        send(secp.at[to], recvg.at[g], ge_send.at[o], ge_recv.at[o], (n, to))
    total = secp[g]
    gse = jnp.concatenate([gsebuf[:, :512], gsebuf[:, 512:]], axis=0)
    for o in range(1, NX * NY):
        source = mod(g - o, NX * NY)
        arrived(recvg.at[source], ge_recv.at[o])
        total = total + recvg[source]
    value = total * (1.0 / 16.0) + gse
    sums = jnp.broadcast_to(jnp.sum(jnp.abs(value), axis=1, keepdims=True), PIECE)
    scale = (sums + pltpu.roll(sums, 4, 0)) * (1.0 / WIDTH)
    piece = jnp.where(value >= 0.0, scale, -scale)
    error = value - piece
    new_gse[:, :512] = error[:4]
    new_gse[:, 512:] = error[4:]

    hz, zz = lax.div(z, 4), lax.rem(z, 4)
    az, bz = y + hz * (x - y), x + hz * (y - x)
    mp[c, hz, az, bz, zz] = piece
    mine = mp.at[c, hz, az, bz, zz]
    for o in range(1, NZ):
        send(mine, mine, z_send.at[o], z_recv.at[o], zdev(o))
    for o in range(1, NZ):
        src = mod(z - o, NZ)
        sh, sz = lax.div(src, 4), lax.rem(src, 4)
        sa, sb = y + sh * (x - y), x + sh * (y - x)
        arrived(mp.at[c, sh, sa, sb, sz], z_recv.at[o])

    def block(h, da, db, core):
        a = mod((y, x)[h] + da, 4)
        b = mod((x, y)[h] + db, 4)
        return mp.at[core, h, a, b]

    def adev(h, d):
        return gdev(0, d) if h == 0 else gdev(d, 0)

    def bdev(h, d):
        return gdev(d, 0) if h == 0 else gdev(0, d)

    def a_spread(h, db):
        ref = block(h, 0, db, c)
        for k, d in enumerate((1, -1)):
            send(ref, ref, a_send.at[h, db, k], a_recv.at[h, db, k], adev(h, d))

    def across(h, da, db):
        ref = block(h, da, db, c)
        send(ref, ref, d_send.at[h, da, db], d_recv.at[h, da, db], partner)

    NEAR = (-1, 1)

    for h in range(2):
        ref = block(h, 0, 0, c)
        for k, d in enumerate((1, -1)):
            send(ref, ref, b_send.at[h, k], b_recv.at[h, k], bdev(h, d))
        a_spread(h, 0)
        across(h, 0, 0)
    for h in range(2):
        for k, d in enumerate((1, -1)):
            ref = block(h, 0, -d, c)
            arrived(ref, b_recv.at[h, k])
            part = ref.at[pl.ds(2 * k, 2)]
            send(part, part, b_send.at[h, 2 + k], b_recv.at[h, 2 + k], bdev(h, d))
            a_spread(h, mod(-d, 4) if isinstance(d, int) is False else (-d) % 4)
            across(h, 0, (-d) % 4)

    def a_forward(h, db):
        for k, d in enumerate((1, -1)):
            ref = block(h, -d, db, c)
            arrived(ref, a_recv.at[h, db, k])
            part = ref.at[pl.ds(2 * k, 2)]
            send(part, part, a_send.at[h, db, 2 + k], a_recv.at[h, db, 2 + k], adev(h, d))
            across(h, (-d) % 4, db)

    for h in range(2):
        a_forward(h, 0)
    for h in range(2):
        ref = block(h, 0, 2, c)
        for k in range(2):
            arrived(ref.at[pl.ds(2 * k, 2)], b_recv.at[h, 2 + k])
        a_spread(h, 2)
        across(h, 0, 2)
    for db in (3, 1, 2):
        for h in range(2):
            a_forward(h, db)
    for db in (0, 3, 1, 2):
        for h in range(2):
            ref = block(h, 2, db, c)
            for k in range(2):
                arrived(ref.at[pl.ds(2 * k, 2)], a_recv.at[h, db, 2 + k])
            across(h, 2, db)
    for db in (0, 3, 1, 2):
        for da in (0, 3, 1, 2):
            for h in range(2):
                arrived(block(h, da, db, 1 - c), d_recv.at[h, da, db])

    for h in range(2):

        def step(t, carry):
            core, rest = lax.div(t, 32), lax.rem(t, 32)
            zq, rest = lax.div(rest, 8), lax.rem(rest, 8)
            px, py = lax.div(rest, 2), lax.rem(rest, 2) * 2
            if h == 0:
                even, odd = mp[core, h, py, px, zq], mp[core, h, py + 1, px, zq]
            else:
                even, odd = mp[core, h, px, py, zq], mp[core, h, px, py + 1, zq]
            at = rows_of(((2 * (4 * h + zq) + core) * 8 + rest) * 8, 8)
            left = jnp.where(low, even, pltpu.roll(odd, 4, 0))
            right = jnp.where(low, pltpu.roll(even, 4, 0), odd)
            new_m[at, :512] = left
            new_m[at, 512:] = right
            new_p[at, :512] = pbuf[at, :512] - vbuf[at, :512] * left
            new_p[at, 512:] = pbuf[at, 512:] - vbuf[at, 512:] * right
            return carry

        lax.fori_loop(0, 64, step, 0)

    for copy in sent:
        copy.wait_send()


def body(gradient, momentum, variance, params, worker_error, server_error, group_worker_error, group_server_error):
    vm, dma = pltpu.VMEM, pltpu.SemaphoreType.DMA
    big = (WIDTH, WIDTH)
    outs = pl.pallas_call(
        kernel,
        out_shape=(
            pltpu.VMEM(big, F32),
            pltpu.VMEM(big, F32),
            pltpu.VMEM(big, F32),
            pltpu.VMEM((SHARD, WIDTH), F32),
            pltpu.VMEM((SHARD, WIDTH), F32),
            pltpu.VMEM((4, WIDTH), F32),
        ),
        in_specs=[pl.BlockSpec(memory_space=pltpu.HBM)] * 8,
        out_specs=[pl.BlockSpec(memory_space=pltpu.VMEM)] * 6,
        scratch_shapes=[
            vm((8, 2 * SHARD, WIDTH), jnp.bfloat16),
            vm((8, 2 * SHARD, WIDTH), F32),
            vm((8, 2 * SHARD, WIDTH), F32),
            vm(big, F32),
            vm(big, F32),
            vm((SHARD, WIDTH), F32),
            vm((SHARD, WIDTH), F32),
            vm((4, WIDTH), F32),
            vm((8, SHARD, WIDTH), F32),
            vm((8, SHARD, WIDTH), F32),
            vm((8, SHARD, WIDTH), F32),
            vm((2, 7, HALF, WIDTH), F32),
            vm((16, *PIECE), F32),
            vm((16, *PIECE), F32),
            vm((2, 2, 4, 4, 4, *PIECE), F32),
            dma((8, 3)), dma((5,)), dma((8,)), dma((8,)),
            dma((2, 7)), dma((2, 7)), dma((16,)), dma((16,)),
            dma((8,)), dma((8,)), dma((2, 4)), dma((2, 4)),
            dma((2, 4, 4)), dma((2, 4, 4)), dma((2, 4, 4)), dma((2, 4, 4)),
        ],
        compiler_params=pltpu.CompilerParams(
            collective_id=0, has_side_effects=True, vmem_limit_bytes=50 * 1024 * 1024
        ),
    )(
        gradient[0, 0], momentum, variance, params, worker_error[0, 0],
        server_error[0], group_worker_error[0], group_server_error,
    )
    new_p, new_m, new_we, new_se, new_gwe, new_gse = outs
    return (new_p, new_m, new_we[None, None], new_se[None], new_gwe[None], new_gse)


def solution(mesh):
    split, shard = P("node", "group", None, None), P("group", "node", None)
    piece = P(("node", "group"), None)
    return jax.shard_map(
        body,
        mesh=mesh,
        in_specs=(split, P(), P(), P(), split, shard, shard, piece),
        out_specs=(P(), P(), split, shard, shard, piece),
        check_vma=False,
    )
```

time: 210 us -> 78.5 us (0.37)
  waiting for transfers between devices: 133 us -> 0 us
  Pallas kernels: 0 us -> 69.7 us
  blocking collectives: 24.8 us -> 0 us
  other arithmetic: 23.5 us -> 0 us
  between operations: 14.1 us -> 0.65 us
  starting transfers between devices: 10.1 us -> 0 us
  local copies, waits for them, and re-layouts: 3.26 us -> 8.05 us
    all_to_all x1 -> x0, waiting for transfers between devices: 93.3 us -> none  [body(): lax.all_to_all(first.reshape(nodes, shard_rows, width), 'node', split_axi...]
    pallas_call x0 -> x1, Pallas kernels: none -> 69.7 us  [body(): pl.pallas_call(kernel, out_shape=(pltpu.VMEM(big, F32), pltpu.VMEM(big, F...]
    all_gather x1 -> x0, waiting for transfers between devices: 40.1 us -> none  [body(): new_momentum = lax.all_gather(shard_momentum, 'node', axis=0, tiled=True)]
    all_to_all x2 -> x0, blocking collectives: 24.8 us -> none  [the longest x1 14 us: body(): lax.all_to_all(second.reshape(groups, shard_rows // groups, width), 'grou...]
    sub x3 -> x0, other arithmetic: 10.5 us -> none  [the longest x1 8.89 us: body(): new_params = params - 0.05 * new_momentum / (jnp.sqrt(variance) + 1e-08)]
    all_to_all x1 -> x0, starting transfers between devices: 10.1 us -> none  [body(): lax.all_to_all(first.reshape(nodes, shard_rows, width), 'node', split_axi...]
    reduce_sum x6 -> x0, other arithmetic: 8.07 us -> none  [the longest x4 5.53 us: compress(): scale = jnp.mean(jnp.abs(values), axis=-1, keepdims=True)]
    unnamed x9 -> x6, local copies, waits for them, and re-layouts: 2.03 us -> 8.05 us
  transfers between devices with their start and end apart: 2 -> 0, of which waited for: 2 -> 0; matrix products, arithmetic and copies ran while one was open for 1% -> 0% of each run, Pallas kernels for 0% -> 0%
where the time goes in v1:
time: 78.5 us; the launch traced here: 78.4 us
  Pallas kernels  69.7 us (89%)
  local copies, waits for them, and re-layouts  8.05 us (10%)
    pallas_call x1, Pallas kernels, body(): pl.pallas_call(kernel, out_shape=(pltpu.VMEM(big, F32), pltpu.VMEM(big, F...  69.7 us
    unnamed x6, local copies, waits for them, and re-layouts  8.05 us

profile of v1, /device:TPU:1, one launch (start us, length us, event | category | flops | bytes accessed | tf_op | source)
XLA Modules:
  0.0 78.4 jit_solution(9462638590102118458)
XLA Ops:
  0.6 69.7 %shard_map.127 = (f32[1024,1024]{1,0:T(8,128)S(1)}, f32[1024,1024]{1,0:T(8,128)S(1)}, f32[1024,1024]{1,0:T(8,128)S(1)}, f32[64,1024]{1,0:T(8,128)S(1)}, f32[64,1024]{1,0:T(8,128)S(1)}, /*index=5*/f32[4,1024]{1,0:T(4,128)S(1)}) custom-call(bf16[1024,1024]{1,0:T(8,128)(2,1)} %bitcast.11, f32[1024,1024]{1,0:T(8,128)} %mom_hbm.1, f32[1024,1024]{1,0:T(8,128)} %var_hbm.1, ...), custom_call_target="tpu_custom_call" | custom-call | tf_op jit(solution)/shard_map/pallas_call | solution.py:315
  70.4 2.0 %copy.20 = f32[1024,1024]{1,0:T(8,128)} copy(f32[1024,1024]{1,0:T(8,128)S(1)} %get-tuple-element.18) | data formatting | bytes 8388608
  72.4 0.6 copy.25
  73.0 0.7 copy.23
  73.7 0.7 copy.24
  74.4 2.0 %copy.21 = f32[1024,1024]{1,0:T(8,128)} copy(f32[1024,1024]{1,0:T(8,128)S(1)} %get-tuple-element.19) | data formatting | bytes 8388608
  76.4 2.0 %copy.22 = f32[1,1,1024,1024]{3,2,1,0:T(8,128)} copy(f32[1,1,1024,1024]{3,2,1,0:T(8,128)S(1)} %bitcast.7) | data formatting | bytes 8388608
